TPU v7x, 16 devices: a 4x2x1 block of a 4x4x8 slice. The times are simulated.
16 devices in a mesh: dp: 2 (over y, z), tp: 8 (over x, core).
Axes of the slice: x: 4, y: 2, z: 1, core: 2. Of those that a mesh axis runs over, the one named last changes fastest.
The devices are a block of a 4x4x8 slice.
Arguments:
- x: bfloat16 [4096, 2048], P('dp'), parts along dimension 0
- dy: bfloat16 [4096, 2048], P('dp'), parts along dimension 0
- gate: bfloat16 [4096, 6144], P('dp', 'tp'), parts along dimension 0
- up: bfloat16 [4096, 6144], P('dp', 'tp'), parts along dimension 0
- w_gate: bfloat16 [2048, 6144], P(None, 'tp')
- w_up: bfloat16 [2048, 6144], P(None, 'tp')
- w_down: bfloat16 [6144, 2048], P('tp')
Outputs:
- output 1: bfloat16 [4096, 2048], P('dp'), parts along dimension 0
- output 2: bfloat16 [4096, 6144], P('dp', 'tp'), parts along dimension 0
- output 3: bfloat16 [4096, 6144], P('dp', 'tp'), parts along dimension 0
- output 4: bfloat16 [12288, 2048], P(('dp', 'tp')), parts along dimension 0
There are 2 independent parts. A program takes and returns all parts, laid end to end along the dimension named above; an argument that names none is the same for every part.
All inputs are finite; a program needn't handle non-finite values.
Results may differ from a plain program's by a relative error of at most 0.012.
Values are sent between devices in bfloat16 or wider.
A program may use at most 768 MiB of HBM per device.

v0:
```python
import jax
import jax.numpy as jnp
from jax import lax
from jax.sharding import PartitionSpec as P


def act(gate, up):
    return jax.nn.silu(gate) * up


def solution(mesh):
    def step(x, dy, gate, up, w_gate, w_up, w_down):
        hidden, back = jax.vjp(act, gate.astype(jnp.float32), up.astype(jnp.float32))
        d_hidden = jnp.dot(dy, w_down.T, preferred_element_type=jnp.float32)
        d_gate, d_up = (g.astype(jnp.bfloat16) for g in back(d_hidden))
        term = jnp.dot(d_gate, w_gate.T, preferred_element_type=jnp.float32) + jnp.dot(d_up, w_up.T, preferred_element_type=jnp.float32)
        dx = lax.psum(term.astype(jnp.bfloat16), "tp")
        dw_gate = jnp.dot(x.T, d_gate, preferred_element_type=jnp.float32)
        dw_up = jnp.dot(x.T, d_up, preferred_element_type=jnp.float32)
        dw_down = jnp.dot(hidden.astype(jnp.bfloat16).T, dy, preferred_element_type=jnp.float32)
        return dx, *(g.astype(jnp.bfloat16) for g in (dw_gate, dw_up, dw_down))

    tokens, columns, rows = P("dp", None), P(None, "tp"), P("tp", None)
    return jax.shard_map(
        step,
        mesh=mesh,
        in_specs=(tokens, tokens, P("dp", "tp"), P("dp", "tp"), columns, columns, rows),
        out_specs=(tokens, P("dp", "tp"), P("dp", "tp"), P(("dp", "tp"), None)),
        check_vma=False,
    )
```

profile of v0, /device:TPU:113, one launch (start us, length us, event | category | flops | bytes accessed | tf_op | source)
XLA Modules:
  0.0 161.9 jit_solution(10429353273489005737)
XLA Ops:
  7.2 0.0 copy-start
  7.2 0.1 all-reduce.2.cloned.1.call-start
  7.3 14.7 %fusion.6 = (bf16[2048,768]{1,0:T(8,128)(2,1)S(1)}, f32[2048,768]{1,0:T(8,128)}) fusion(bf16[2048,768]{1,0:T(8,128)(2,1)} %param.9, bf16[2048,768]{1,0:T(8,128)(2,1)} %param.10, bf16[2048,2048]{1,0:T(8,128)(2,1)} %param.8, bf16[768,2048]{1,0:T(8,128)(2,1)} %param.13), kind=kOutput, calls=%fused_computation.13 | convolution fusion | flops 6462898176 | bytes 27262976 | tf_op jit(solution)/shard_map/dot_general | solution.py:14
  21.9 0.0 copy-start.2
  21.9 0.0 copy-done
  21.9 9.6 %fusion.11 = f32[2048,2048]{1,0:T(8,128)} fusion(bf16[2048,768]{1,0:T(8,128)(2,1)S(1)} %get-tuple-element.8, bf16[2048,768]{1,0:T(8,128)(2,1)S(1)} %copy-done), kind=kOutput, calls=%fused_computation.21 | convolution fusion | flops 6442450944 | bytes 23068672 | tf_op jit(solution)/shard_map/dot_general | solution.py:16
  31.5 0.0 copy-done.2
  31.5 16.4 %add_convert_fusion = bf16[2048,2048]{1,0:T(8,128)(2,1)} fusion(f32[2048,2048]{1,0:T(8,128)} %fusion.11, bf16[2048,768]{1,0:T(8,128)(2,1)} %param.12, f32[2048,768]{1,0:T(8,128)} %get-tuple-element.9, bf16[2048,768]{1,0:T(8,128)(2,1)} %param.9), kind=kOutput, calls=%fused_computation | convolution fusion | flops 6461849600 | bytes 37748736 | tf_op jit(solution)/shard_map/dot_general | solution.py:16
  48.0 0.1 all-reduce.2.cloned.1.call-update
  48.0 10.1 %fusion.8 = bf16[2048,768]{0,1:T(8,128)(2,1)S(1)} fusion(bf16[2048,768]{1,0:T(8,128)(2,1)} %copy-done.2, bf16[2048,2048]{1,0:T(8,128)(2,1)} %param.7), kind=kOutput, calls=%fused_computation.18 | convolution fusion | flops 6444023808 | bytes 14680064 | tf_op jit(solution)/shard_map/dot_general | solution.py:18
  58.2 2.8 %copy.11 = bf16[2048,768]{1,0:T(8,128)(2,1)} copy(bf16[2048,768]{0,1:T(8,128)(2,1)S(1)} %fusion.8) | data formatting | bytes 6291456
  61.0 12.4 %fusion.9 = bf16[2048,768]{0,1:T(8,128)(2,1)S(1)} fusion(bf16[2048,2048]{1,0:T(8,128)(2,1)} %param.7, f32[2048,768]{1,0:T(8,128)} %get-tuple-element.9, bf16[2048,768]{1,0:T(8,128)(2,1)} %param.9), kind=kOutput, calls=%fused_computation.19 | convolution fusion | flops 6455033856 | bytes 20971520 | tf_op jit(solution)/shard_map/dot_general | solution.py:19
  73.4 2.8 %copy.12 = bf16[2048,768]{1,0:T(8,128)(2,1)} copy(bf16[2048,768]{0,1:T(8,128)(2,1)S(1)} %fusion.9) | data formatting | bytes 6291456
  76.2 0.0 copy-start.1
  76.2 13.3 %convolution_convert_fusion = bf16[768,2048]{1,0:T(8,128)(2,1)} fusion(bf16[2048,2048]{1,0:T(8,128)(2,1)} %param.8, bf16[2048,768]{1,0:T(8,128)(2,1)} %param.10, bf16[2048,768]{1,0:T(8,128)(2,1)} %param.9), kind=kOutput, calls=%fused_computation.15 | convolution fusion | flops 6456606720 | bytes 17825792 | tf_op jit(solution)/shard_map/dot_general | solution.py:20
  89.5 57.1 %all-reduce.2.cloned.1.call-done = bf16[2048,2048]{1,0:T(8,128)(2,1)} async-done(((bf16[2048,2048]{1,0:T(8,128)(2,1)}), bf16[2048,2048]{1,0:T(8,128)(2,1)}) %all-reduce.2.cloned.1.call-update) | async-done | bytes 8388624 | tf_op jit(solution)/shard_map/psum | solution.py:17
  146.6 8.4 %copy.14 = bf16[2048,2048]{1,0:T(8,128)(2,1)} copy(bf16[2048,2048]{1,0:T(8,128)(2,1)} %all-reduce.2.cloned.1.call-done) | data formatting | bytes 16777216
  155.1 0.0 copy-done.1
Async XLA Ops:
  7.2 14.8 %copy-start = (bf16[2048,768]{1,0:T(8,128)(2,1)S(1)}, bf16[2048,768]{1,0:T(8,128)(2,1)}, u32[]{:S(2)}) copy-start(bf16[2048,768]{1,0:T(8,128)(2,1)} %param.11) | copy-start | bytes 9437188
  7.2 139.4 %all-reduce.2.cloned.1.call-start = ((), (), s32[]{:S(2)}) async-start(), calls=%async_computation | async-start | bytes 16777216 | tf_op jit(solution)/shard_map/psum | solution.py:17
  21.9 9.6 %copy-start.2 = (bf16[2048,768]{1,0:T(8,128)(2,1)}, bf16[2048,768]{1,0:T(8,128)(2,1)S(1)}, u32[]{:S(2)}) copy-start(bf16[2048,768]{1,0:T(8,128)(2,1)S(1)} %get-tuple-element.8) | copy-start | bytes 9437188
  76.2 78.8 %copy-start.1 = (bf16[2048,768]{1,0:T(8,128)(2,1)S(1)}, bf16[2048,768]{1,0:T(8,128)(2,1)}, u32[]{:S(2)}) copy-start(bf16[2048,768]{1,0:T(8,128)(2,1)} %param.11) | copy-start | bytes 9437188
Sparse Core Ops, SparseCore 0:
  48.2 98.4 all-reduce.1
where the time goes:
time: 162 us
  matrix products  76.6 us (47%)
  waiting for transfers between devices  57.1 us (35%)
  between operations  14.1 us (9%)
  local copies, waits for them, and re-layouts  14 us (9%)
    psum x1, waiting for transfers between devices, step(): dx = lax.psum(term.astype(jnp.bfloat16), 'tp')  57.1 us
    dot_general x1, matrix products, step(): jnp.dot(d_up, w_up.T, preferred_element_type=jnp.float32)  16.4 us
    dot_general x1, matrix products, step(): d_hidden = jnp.dot(dy, w_down.T, preferred_element_type=jnp.float32)  14.7 us
    unnamed x9, local copies, waits for them, and re-layouts  14 us
    dot_general x1, matrix products, step(): jnp.dot(hidden.astype(jnp.bfloat16).T, dy, preferred_element_type=jnp.flo...  13.3 us
    dot_general x1, matrix products, step(): dw_up = jnp.dot(x.T, d_up, preferred_element_type=jnp.float32)  12.4 us
    dot_general x1, matrix products, step(): dw_gate = jnp.dot(x.T, d_gate, preferred_element_type=jnp.float32)  10.1 us
    dot_general x1, matrix products, step(): jnp.dot(d_gate, w_gate.T, preferred_element_type=jnp.float32)  9.59 us
  transfers between devices with their start and end apart: 1, of which 1 were waited for; matrix products, arithmetic and copies ran while one was open for 26% of the time, Pallas kernels for 0%

commit v1 on v0

v1 whole, which is shorter than its diff:
```python
import functools

import jax
import jax.numpy as jnp
from jax import lax
from jax.experimental import pallas as pl
from jax.experimental.pallas import tpu as pltpu
from jax.sharding import PartitionSpec as P

BF16, F32 = jnp.bfloat16, jnp.float32
ANY = pl.BlockSpec(memory_space=pl.ANY)
VMEM = pl.BlockSpec(memory_space=pltpu.VMEM)
PIECES = 4
TILE = 256


def dot(a, b, a_dim, b_dim):
    return lax.dot_general(a, b, (((a_dim,), (b_dim,)), ((), ())), preferred_element_type=F32)


def work(
    chips, x, dy, gate, up, w_gate, w_up, w_down, dx, wg, wu, wd,
    own, got, ring, mate, dys, dgs, dus, hid, gs, us, xs,
    load, wload, xload, pair_s, pair_r, rs_s, rs_r, ag_s, ag_r, fin_s, fin_r,
):
    rows, width = dx.shape
    hidden = wd.shape[0]
    block = rows // (4 * chips)
    part = width // PIECES
    t = lax.axis_index("tp")
    k, c = t // 2, t % 2
    right = {"tp": (k + 1) % chips * 2 + c}
    left = {"tp": (k + chips - 1) % chips * 2 + c}
    partner = {"tp": k * 2 + 1 - c}
    ways = (right, left)

    def origin(d, hops):
        return (k + chips - hops) % chips if d == 0 else (k + hops) % chips

    def row(chunk, d, core):
        return pl.multiple_of((chunk * 4 + d * 2 + core) * block, block)

    def segments(s):
        todo = [(k + 2 * chips - 1 - s) % chips, (k + 1 + s) % chips]
        return [row(todo[d], d, core) for core in (c, 1 - c) for d in (0, 1)]

    def load_dy(s):
        for i, r in enumerate(segments(s)):
            pltpu.make_async_copy(
                dy.at[pl.ds(r, block)], dys.at[pl.ds((4 * s + i) * block, block)], load.at[0, s]
            ).start()

    def load_act(s):
        for i, r in enumerate(segments(s)):
            for n, (src, dst) in enumerate(((gate, gs), (up, us))):
                pltpu.make_async_copy(
                    src.at[pl.ds(r, block)], dst.at[s % 2, pl.ds(i * block, block)], load.at[1 + n, s]
                ).start()

    def load_x(b):
        for s in range(chips):
            for i, r in enumerate(segments(s)):
                pltpu.make_async_copy(
                    x.at[pl.ds(r, block), pl.ds(b * part, part)],
                    xs.at[b % 2, pl.ds((4 * s + i) * block, block)],
                    xload.at[b],
                ).start()

    def weights(src, dst, n, sem):
        size = src.shape[0] // n
        return [
            pltpu.make_async_copy(src.at[pl.ds(i * size, size)], dst.at[pl.ds(i * size, size)], wload.at[sem, i])
            for i in range(n)
        ]

    wd_loads = weights(w_down, wd, hidden // TILE, 0)
    wg_loads = weights(w_gate, wg, PIECES, 1)
    wu_loads = weights(w_up, wu, PIECES, 2)
    load_dy(0)
    for copy in wd_loads:
        copy.start()
    load_act(0)
    for a, b in zip(wg_loads, wu_loads):
        a.start()
        b.start()
    for s in range(1, chips):
        load_dy(s)
    load_act(1)
    load_x(0)
    load_x(1)

    barrier = pltpu.get_barrier_semaphore()
    for other in (right, left, partner):
        pl.semaphore_signal(barrier, inc=1, device_id=other)
    pl.semaphore_wait(barrier, 3)

    def remote(src, dst, send, recv, to):
        return pltpu.make_async_remote_copy(src_ref=src, dst_ref=dst, send_sem=send, recv_sem=recv, device_id=to)

    def pair(s, q):
        at = (pl.ds(0, 2 * block), pl.ds(q * part, part))
        return remote(mate.at[s % 2, *at], got.at[s, *at], pair_s.at[s, q], pair_r.at[s, q], partner)

    def reduce(d, s, q):
        cols = pl.ds(q * part, part)
        return remote(
            got.at[s, pl.ds(d * block, block), cols], ring.at[d, s, :, cols], rs_s.at[d, s, q], rs_r.at[d, s, q], ways[d]
        )

    def gather(d, hops, q):
        at = dx.at[pl.ds(row(origin(d, hops), d, c), block), pl.ds(q * part, part)]
        return remote(at, at, ag_s.at[d, hops, q], ag_r.at[d, hops, q], ways[d])

    def share(d, hops, q):
        at = dx.at[pl.ds(row(origin(d, hops), d, c), block), pl.ds(q * part, part)]
        return remote(at, at, fin_s.at[d, hops, q], fin_r.at[d, hops, q], partner)

    def pass_on(s, q):
        cols = pl.ds(q * part, part)
        pair(s, q).wait_recv()
        for d in (0, 1):
            band = pl.ds(d * block, block)
            total = own[s, band, cols] + got[s, band, cols].astype(F32)
            if s > 0:
                reduce(d, s - 1, q).wait_recv()
                total = total + ring[d, s - 1, :, cols].astype(F32)
            if s < chips - 1:
                got[s, band, cols] = total.astype(BF16)
            else:
                dx[pl.ds(row(k, d, c), block), cols] = total.astype(BF16)
        for d in (0, 1):
            if s < chips - 1:
                reduce(d, s, q).start()
            else:
                gather(d, 0, q).start()
        if s == chips - 1:
            for d in (0, 1):
                share(d, 0, q).start()

    def forward(hops, q):
        for d in (0, 1):
            gather(d, hops - 1, q).wait_recv()
            if hops < chips - 1:
                gather(d, hops, q).start()
            share(d, hops, q).start()

    for s in range(chips):
        here = pl.ds(4 * s * block, 4 * block)
        pltpu.make_async_copy(dy.at[pl.ds(0, 4 * block)], dys.at[here], load.at[0, s]).wait()

        def act_back(i, s=s, here=here):
            cols = pl.ds(pl.multiple_of(i * TILE, TILE), TILE)
            dh = dot(dys[here], wd[cols, :], 1, 1)
            g = gs[s % 2, :, cols].astype(F32)
            u = us[s % 2, :, cols].astype(F32)
            sig = lax.logistic(g)
            silu = g * sig
            ct = dh * u
            hid[here, cols] = (silu * u).astype(BF16)
            dus[here, cols] = (dh * silu).astype(BF16)
            dgs[here, cols] = (ct * sig + (ct * g) * (sig * (1.0 - sig))).astype(BF16)

        def wait_act(s=s):
            pltpu.make_async_copy(gate.at[pl.ds(0, 4 * block)], gs.at[s % 2], load.at[1, s]).wait()
            pltpu.make_async_copy(up.at[pl.ds(0, 4 * block)], us.at[s % 2], load.at[2, s]).wait()

        if s == 0:
            for i in range(hidden // TILE):
                wd_loads[i].wait()
                if i == 0:
                    wait_act()
                act_back(i)
        else:
            wait_act()
            pl.loop(0, hidden // TILE)(act_back)
        if s + 2 < chips:
            load_act(s + 2)

        for q in range(PIECES):
            if s == 0:
                wg_loads[q].wait()
                wu_loads[q].wait()
            if s >= 2:
                pair(s - 2, q).wait_send()

            def term(i, s=s, q=q, here=here):
                cols = pl.ds(pl.multiple_of(q * part + i * TILE, TILE), TILE)
                v = dot(dgs[here, :], wg[cols, :], 1, 1) + dot(dus[here, :], wu[cols, :], 1, 1)
                own[s, :, cols] = v[: 2 * block]
                mate[s % 2, :, cols] = v[2 * block :].astype(BF16)

            pl.loop(0, part // TILE)(term)
            pair(s, q).start()
            if q > 0:
                pass_on(s, q - 1)
        pass_on(s, PIECES - 1)

    events = [(hops, q) for hops in range(1, chips) for q in range(PIECES)]

    def columns_of(i):
        return pl.ds(pl.multiple_of(i * TILE, TILE), TILE)

    for b in range(PIECES):
        band = pl.ds(b * part, part)
        pltpu.make_async_copy(x.at[:, band], xs.at[b % 2], xload.at[b]).wait()

        @pl.loop(0, hidden // TILE)
        def _(i, b=b, band=band):
            wg[band, columns_of(i)] = dot(xs[b % 2], dgs[:, columns_of(i)], 0, 0).astype(BF16)

        if b > 0:
            forward(*events.pop(0))

        @pl.loop(0, hidden // TILE)
        def _(i, b=b, band=band):
            wu[band, columns_of(i)] = dot(xs[b % 2], dus[:, columns_of(i)], 0, 0).astype(BF16)

        if b + 2 < PIECES:
            load_x(b + 2)
        forward(*events.pop(0))

        @pl.loop(0, part // TILE)
        def _(i, b=b):
            cols = pl.ds(pl.multiple_of(b * part + i * TILE, TILE), TILE)
            wd[:, cols] = dot(hid[...], dys[:, cols], 0, 0).astype(BF16)

    while events:
        forward(*events.pop(0))

    for q in range(PIECES):
        for s in range(max(chips - 2, 0), chips):
            pair(s, q).wait_send()
        for d in (0, 1):
            for s in range(chips - 1):
                reduce(d, s, q).wait_send()
                gather(d, s, q).wait_send()
            for s in range(chips):
                share(d, s, q).wait_send()
                share(d, s, q).wait_recv()


def store(*refs):
    n = (len(refs) - 1) // 2
    sems = refs[-1]
    for i, (src, dst) in enumerate(zip(refs[:n], refs[n:-1])):
        size = src.shape[0] // PIECES
        for p in range(PIECES):
            at = pl.ds(p * size, size)
            pltpu.make_async_copy(src.at[at], dst.at[at], sems.at[i]).start()
    for i, (src, dst) in enumerate(zip(refs[:n], refs[n:-1])):
        pltpu.make_async_copy(src, dst, sems.at[i]).wait()


def solution(mesh):
    chips = mesh.shape["tp"] // 2

    def step(x, dy, gate, up, w_gate, w_up, w_down):
        rows, width = x.shape
        hidden = gate.shape[1]
        block = rows // (4 * chips)
        shapes = ((rows, width), w_gate.shape, w_up.shape, w_down.shape)
        dma = pltpu.SemaphoreType.DMA
        outs = pl.pallas_call(
            functools.partial(work, chips),
            name="work",
            out_shape=[pltpu.VMEM(s, BF16) for s in shapes],
            in_specs=[ANY] * 7,
            out_specs=[VMEM] * 4,
            scratch_shapes=[
                pltpu.VMEM((chips, 2 * block, width), F32),
                pltpu.VMEM((chips, 2 * block, width), BF16),
                pltpu.VMEM((2, chips - 1, block, width), BF16),
                pltpu.VMEM((2, 2 * block, width), BF16),
                pltpu.VMEM((rows, width), BF16),
                pltpu.VMEM((rows, hidden), BF16),
                pltpu.VMEM((rows, hidden), BF16),
                pltpu.VMEM((rows, hidden), BF16),
                pltpu.VMEM((2, 4 * block, hidden), BF16),
                pltpu.VMEM((2, 4 * block, hidden), BF16),
                pltpu.VMEM((2, rows, width // PIECES), BF16),
                dma((3, chips)),
                dma((3, PIECES)),
                dma((PIECES,)),
                dma((chips, PIECES)),
                dma((chips, PIECES)),
                dma((2, chips - 1, PIECES)),
                dma((2, chips - 1, PIECES)),
                dma((2, chips - 1, PIECES)),
                dma((2, chips - 1, PIECES)),
                dma((2, chips, PIECES)),
                dma((2, chips, PIECES)),
            ],
            compiler_params=pltpu.CompilerParams(
                collective_id=0, has_side_effects=True, vmem_limit_bytes=46 * 2**20
            ),
        )(x, dy, gate, up, w_gate, w_up, w_down)
        return pl.pallas_call(
            store,
            name="store",
            out_shape=[jax.ShapeDtypeStruct(s, BF16) for s in shapes],
            in_specs=[VMEM] * 4,
            out_specs=[ANY] * 4,
            scratch_shapes=[dma((4,))],
            compiler_params=pltpu.CompilerParams(vmem_limit_bytes=2**20),
        )(*(pltpu.with_memory_space_constraint(o, pltpu.VMEM) for o in outs))

    tokens, columns, down = P("dp", None), P(None, "tp"), P("tp", None)
    return jax.shard_map(
        step,
        mesh=mesh,
        in_specs=(tokens, tokens, P("dp", "tp"), P("dp", "tp"), columns, columns, down),
        out_specs=(tokens, P("dp", "tp"), P("dp", "tp"), P(("dp", "tp"), None)),
        check_vma=False,
    )
```

time: 162 us -> 94.1 us (0.58)
  Pallas kernels: 0 us -> 93.2 us
  matrix products: 76.6 us -> 0 us
  waiting for transfers between devices: 57.1 us -> 0 us
  local copies, waits for them, and re-layouts: 14 us -> 0 us
  between operations: 14.1 us -> 0.82 us
    pallas_call x0 -> x2, Pallas kernels: none -> 93.2 us  [the longest x1 87 us: step(): pl.pallas_call(functools.partial(work, chips), name='work', out_shape=[pl...]
    dot_general x6 -> x0, matrix products: 76.6 us -> none  [the longest x1 16.4 us: step(): jnp.dot(d_up, w_up.T, preferred_element_type=jnp.float32)]
    psum x1 -> x0, waiting for transfers between devices: 57.1 us -> none  [step(): dx = lax.psum(term.astype(jnp.bfloat16), 'tp')]
    unnamed x9 -> x0, local copies, waits for them, and re-layouts: 14 us -> none
  transfers between devices with their start and end apart: 1 -> 0, of which waited for: 1 -> 0; matrix products, arithmetic and copies ran while one was open for 26% -> 0% of each run, Pallas kernels for 0% -> 0%
where the time goes in v1:
time: 94.1 us; the launch traced here: 94 us
  Pallas kernels  93.2 us (99%)
    pallas_call x1, Pallas kernels, step(): pl.pallas_call(functools.partial(work, chips), name='work', out_shape=[pl...  87 us
    pallas_call x1, Pallas kernels, step(): pl.pallas_call(store, name='store', out_shape=[jax.ShapeDtypeStruct(s, BF...  6.16 us

profile of v1, /device:TPU:113, one launch (start us, length us, event | category | flops | bytes accessed | tf_op | source)
XLA Modules:
  0.0 94.0 jit_solution(16023640015666089947)
XLA Ops:
  0.6 87.0 %work.1 = (bf16[2048,2048]{1,0:T(8,128)(2,1)S(1)}, bf16[2048,768]{1,0:T(8,128)(2,1)S(1)}, bf16[2048,768]{1,0:T(8,128)(2,1)S(1)}, bf16[768,2048]{1,0:T(8,128)(2,1)S(1)}) custom-call(bf16[2048,2048]{1,0:T(8,128)(2,1)} %x.1, bf16[2048,2048]{1,0:T(8,128)(2,1)} %dy.1, bf16[2048,768]{1,0:T(8,128)(2,1)} %gate.1, bf16[2048,768]{1,0:T(8,128)(2,1)} %up.1, ...), custom_call_target="tpu_custom_call" | custom-call | tf_op jit(solution)/shard_map/work/pallas_call | solution.py:263
  87.6 6.2 %store.1 = (bf16[2048,2048]{1,0:T(8,128)(2,1)}, bf16[2048,768]{1,0:T(8,128)(2,1)}, bf16[2048,768]{1,0:T(8,128)(2,1)}, bf16[768,2048]{1,0:T(8,128)(2,1)}) custom-call(bf16[2048,2048]{1,0:T(8,128)(2,1)S(1)} %get-tuple-element.8.refs_0_, bf16[2048,768]{1,0:T(8,128)(2,1)S(1)} %get-tuple-element.9.refs_1_, bf16[2048,768]{1,0:T(8,128)(2,1)S(1)} %get-tuple-element.10.refs_2_, ...), custom_call_target="tpu_custom_call" | custom-call | tf_op jit(solution)/shard_map/store/pallas_call | solution.py:297

commit v2 on v1

v2 whole, which is shorter than its diff:
```python
import functools

import jax
import jax.numpy as jnp
from jax import lax
from jax.experimental import pallas as pl
from jax.experimental.pallas import tpu as pltpu
from jax.sharding import PartitionSpec as P

BF16, F32 = jnp.bfloat16, jnp.float32
ANY = pl.BlockSpec(memory_space=pl.ANY)
VMEM = pl.BlockSpec(memory_space=pltpu.VMEM)
PIECES = 4
TILE = 256


def dot(a, b, a_dim, b_dim):
    return lax.dot_general(a, b, (((a_dim,), (b_dim,)), ((), ())), preferred_element_type=F32)


def work(
    chips, x, dy, gate, up, w_gate, w_up, w_down, dx, wg, wu, wd,
    own, got, ring, mate, dys, dgu, hid, gs, us, wgu,
    load, wload, xload, pair_s, pair_r, rs_s, rs_r, ag_s, ag_r, fin_s, fin_r,
):
    rows, width = dx.shape
    hidden = wd.shape[0]
    block = rows // (4 * chips)
    part = width // PIECES
    t = lax.axis_index("tp")
    k, c = t // 2, t % 2
    right = {"tp": (k + 1) % chips * 2 + c}
    left = {"tp": (k + chips - 1) % chips * 2 + c}
    partner = {"tp": k * 2 + 1 - c}
    ways = (right, left)

    def origin(d, hops):
        return (k + chips - hops) % chips if d == 0 else (k + hops) % chips

    def row(chunk, d, core):
        return pl.multiple_of((chunk * 4 + d * 2 + core) * block, block)

    units = [(0, 0), (0, 1)] + [(s, 0) for s in range(1, chips)]

    def high(s):
        return block // 2 if s == 0 else block

    def halves(s):
        return (0, 1) if s == 0 else (0,)

    def number(s, h):
        return units.index((s, h))

    def begin(s, h):
        return 4 * (s * block + h * high(s))

    def segments(s, h):
        todo = [(k + 2 * chips - 1 - s) % chips, (k + 1 + s) % chips]
        return [row(todo[d], d, core) + h * high(s) for core in (c, 1 - c) for d in (0, 1)]

    def load_dy(s, h):
        n = high(s)
        for i, r in enumerate(segments(s, h)):
            pltpu.make_async_copy(
                dy.at[pl.ds(r, n)], dys.at[pl.ds(begin(s, h) + i * n, n)], load.at[0, number(s, h)]
            ).start()

    def load_act(s, h):
        n = high(s)
        for i, r in enumerate(segments(s, h)):
            for m, (src, dst) in enumerate(((gate, gs), (up, us))):
                pltpu.make_async_copy(
                    src.at[pl.ds(r, n)],
                    dst.at[s % 2, pl.ds((h * 4 + i) * n, n)],
                    load.at[1 + m, number(s, h)],
                ).start()

    def load_x(b):
        for s, h in units:
            n = high(s)
            for i, r in enumerate(segments(s, h)):
                pltpu.make_async_copy(
                    x.at[pl.ds(r, n), pl.ds(b * part, part)],
                    wgu.at[pl.ds(begin(s, h) + i * n, n), pl.ds(b % 2 * part, part)],
                    xload.at[b],
                ).start()

    def weights(q):
        band = pl.ds(q * part, part)
        return [
            pltpu.make_async_copy(src.at[band], wgu.at[band, pl.ds(m * hidden, hidden)], wload.at[m, q])
            for m, src in enumerate((w_gate, w_up))
        ]

    def start(copies):
        for copy in copies:
            copy.start()

    def weights_down(i):
        n = TILE // PIECES
        for j in range(PIECES):
            band = pl.ds(i * TILE + j * n, n)
            pltpu.make_async_copy(w_down.at[band], wd.at[band], wload.at[2, i]).start()

    def wait_weights_down(i):
        band = pl.ds(i * TILE, TILE)
        pltpu.make_async_copy(w_down.at[band], wd.at[band], wload.at[2, i]).wait()

    load_act(0, 0)
    load_dy(0, 0)
    for i in range(hidden // TILE):
        weights_down(i)
    start(weights(0))

    barrier = pltpu.get_barrier_semaphore()
    for other in (right, left, partner):
        pl.semaphore_signal(barrier, inc=1, device_id=other)

    def remote(src, dst, send, recv, to):
        return pltpu.make_async_remote_copy(src_ref=src, dst_ref=dst, send_sem=send, recv_sem=recv, device_id=to)

    def pair(s, h, q):
        at = (pl.ds(h * 2 * high(s), 2 * high(s)), pl.ds(q * part, part))
        u = number(s, h)
        return remote(mate.at[s % 2, *at], got.at[s, *at], pair_s.at[u, q], pair_r.at[u, q], partner)

    def reduce(d, s, h, q):
        cols = pl.ds(q * part, part)
        n, u = high(s), number(s, h)
        return remote(
            got.at[s, pl.ds((h * 2 + d) * n, n), cols],
            ring.at[d, s, pl.ds(h * n, n), cols],
            rs_s.at[d, u, q],
            rs_r.at[d, u, q],
            ways[d],
        )

    def gather(d, hops, q):
        at = dx.at[pl.ds(row(origin(d, hops), d, c), block), pl.ds(q * part, part)]
        return remote(at, at, ag_s.at[d, hops, q], ag_r.at[d, hops, q], ways[d])

    def share(d, hops, q):
        at = dx.at[pl.ds(row(origin(d, hops), d, c), block), pl.ds(q * part, part)]
        return remote(at, at, fin_s.at[d, hops, q], fin_r.at[d, hops, q], partner)

    def pass_on(s, h, q):
        cols = pl.ds(q * part, part)
        n = high(s)
        pair(s, h, q).wait_recv()
        for d in (0, 1):
            band = pl.ds((h * 2 + d) * n, n)
            total = own[s, band, cols] + got[s, band, cols].astype(F32)
            if s > 0:
                for before in halves(s - 1):
                    reduce(d, s - 1, before, q).wait_recv()
                total = total + ring[d, s - 1, :, cols].astype(F32)
            if s < chips - 1:
                got[s, band, cols] = total.astype(BF16)
            else:
                dx[pl.ds(row(k, d, c), block), cols] = total.astype(BF16)
        for d in (0, 1):
            if s < chips - 1:
                reduce(d, s, h, q).start()
            else:
                gather(d, 0, q).start()
        if s == chips - 1:
            for d in (0, 1):
                share(d, 0, q).start()

    def forward(hops, q):
        for d in (0, 1):
            gather(d, hops - 1, q).wait_recv()
            if hops < chips - 1:
                gather(d, hops, q).start()
            share(d, hops, q).start()

    waiting = []
    for s, h in units:
        n = high(s)
        here = pl.ds(begin(s, h), 4 * n)
        there = pl.ds(h * 4 * n, 4 * n)
        u = number(s, h)

        def gates(i, s=s, here=here, there=there):
            cols = pl.ds(pl.multiple_of(i * TILE, TILE), TILE)
            g = gs[s % 2, there, cols].astype(F32)
            v = us[s % 2, there, cols].astype(F32)
            sig = lax.logistic(g)
            silu = g * sig
            hid[here, cols] = (silu * v).astype(BF16)
            return silu, sig + g * (sig * (1.0 - sig)), v

        def back(i, silu, slope, v, here=here):
            cols = pl.ds(pl.multiple_of(i * TILE, TILE), TILE)
            up_cols = pl.ds(pl.multiple_of(hidden + i * TILE, TILE), TILE)
            dh = dot(dys[here], wd[cols, :], 1, 1)
            dgu[here, cols] = (dh * v * slope).astype(BF16)
            dgu[here, up_cols] = (dh * silu).astype(BF16)

        for m, (src, dst) in enumerate(((gate, gs), (up, us))):
            pltpu.make_async_copy(src.at[pl.ds(0, 4 * n)], dst.at[s % 2, there], load.at[1 + m, u]).wait()
        if u == 0:
            for i in range(hidden // TILE):
                silu, slope, _ = gates(i)
                own[chips - 1, pl.ds(0, 4 * n), pl.ds(i * TILE, TILE)] = silu
                own[chips - 1, pl.ds(0, 4 * n), pl.ds(hidden + i * TILE, TILE)] = slope
            pltpu.make_async_copy(dy.at[pl.ds(0, 4 * n)], dys.at[here], load.at[0, u]).wait()
            for i in range(hidden // TILE):
                wait_weights_down(i)
                if i > 0:
                    start(weights(i))
                silu = own[chips - 1, pl.ds(0, 4 * n), pl.ds(i * TILE, TILE)]
                slope = own[chips - 1, pl.ds(0, 4 * n), pl.ds(hidden + i * TILE, TILE)]
                back(i, silu, slope, us[0, there, pl.ds(i * TILE, TILE)].astype(F32))
            for q in range(hidden // TILE, PIECES):
                start(weights(q))
        else:
            pltpu.make_async_copy(dy.at[pl.ds(0, 4 * n)], dys.at[here], load.at[0, u]).wait()
            pl.loop(0, hidden // TILE)(lambda i: back(i, *gates(i)))
        if u + 1 < len(units):
            load_dy(*units[u + 1])
            load_act(*units[u + 1])

        for q in range(PIECES):
            if u == 0:
                for copy in weights(q):
                    copy.wait()
            if s >= 2:
                for before in halves(s - 2):
                    pair(s - 2, before, q).wait_send()
            cols = pl.ds(q * part, part)
            v = dot(dgu[here, :], wgu[cols, :], 1, 1)
            mate[s % 2, pl.ds(h * 2 * n, 2 * n), cols] = v[2 * n :].astype(BF16)
            if u == 0 and q == 0:
                pl.semaphore_wait(barrier, 3)
            pair(s, h, q).start()
            own[s, pl.ds(h * 2 * n, 2 * n), cols] = v[: 2 * n]
            waiting.append((s, h, q))
            while len(waiting) > (2 if s == 0 else 1):
                pass_on(*waiting.pop(0))
        if (s, h) == units[-1]:
            load_x(0)
            load_x(1)
    while waiting:
        pass_on(*waiting.pop(0))

    events = [(hops, q) for hops in range(1, chips) for q in range(PIECES)]

    for b in range(PIECES):
        band = pl.ds(b * part, part)
        slot = pl.ds(b % 2 * part, part)

        @pl.loop(0, part // TILE)
        def _(i, b=b):
            cols = pl.ds(pl.multiple_of(b * part + i * TILE, TILE), TILE)
            wd[:, cols] = dot(hid[...], dys[:, cols], 0, 0).astype(BF16)

        if b > 0:
            forward(*events.pop(0))
        pltpu.make_async_copy(x.at[:, band], wgu.at[:, slot], xload.at[b]).wait()

        for m, out in enumerate((wg, wu)):

            @pl.loop(0, hidden // TILE)
            def _(i, m=m, out=out, band=band, slot=slot):
                cols = pl.ds(pl.multiple_of(i * TILE, TILE), TILE)
                from_cols = pl.ds(pl.multiple_of(m * hidden + i * TILE, TILE), TILE)
                out[band, cols] = dot(wgu[:, slot], dgu[:, from_cols], 0, 0).astype(BF16)

            if m == 0:
                forward(*events.pop(0))
        if b + 2 < PIECES:
            load_x(b + 2)

    while events:
        forward(*events.pop(0))

    for q in range(PIECES):
        for s, h in units:
            if s >= chips - 2:
                pair(s, h, q).wait_send()
            if s < chips - 1:
                for d in (0, 1):
                    reduce(d, s, h, q).wait_send()
        for d in (0, 1):
            for hops in range(chips - 1):
                gather(d, hops, q).wait_send()
            for hops in range(chips):
                share(d, hops, q).wait_send()
                share(d, hops, q).wait_recv()


def store(*refs):
    n = (len(refs) - 1) // 2
    sems = refs[-1]
    for i, (src, dst) in enumerate(zip(refs[:n], refs[n:-1])):
        size = src.shape[0] // PIECES
        for p in range(PIECES):
            at = pl.ds(p * size, size)
            pltpu.make_async_copy(src.at[at], dst.at[at], sems.at[i]).start()
    for i, (src, dst) in enumerate(zip(refs[:n], refs[n:-1])):
        pltpu.make_async_copy(src, dst, sems.at[i]).wait()


def solution(mesh):
    chips = mesh.shape["tp"] // 2

    def step(x, dy, gate, up, w_gate, w_up, w_down):
        rows, width = x.shape
        hidden = gate.shape[1]
        block = rows // (4 * chips)
        shapes = ((rows, width), w_gate.shape, w_up.shape, w_down.shape)
        dma = pltpu.SemaphoreType.DMA
        outs = pl.pallas_call(
            functools.partial(work, chips),
            name="work",
            out_shape=[pltpu.VMEM(s, BF16) for s in shapes],
            in_specs=[ANY] * 7,
            out_specs=[VMEM] * 4,
            scratch_shapes=[
                pltpu.VMEM((chips, 2 * block, width), F32),
                pltpu.VMEM((chips, 2 * block, width), BF16),
                pltpu.VMEM((2, chips - 1, block, width), BF16),
                pltpu.VMEM((2, 2 * block, width), BF16),
                pltpu.VMEM((rows, width), BF16),
                pltpu.VMEM((rows, 2 * hidden), BF16),
                pltpu.VMEM((rows, hidden), BF16),
                pltpu.VMEM((2, 4 * block, hidden), BF16),
                pltpu.VMEM((2, 4 * block, hidden), BF16),
                pltpu.VMEM((width, 2 * hidden), BF16),
                dma((3, chips + 1)),
                dma((3, PIECES)),
                dma((PIECES,)),
                dma((chips + 1, PIECES)),
                dma((chips + 1, PIECES)),
                dma((2, chips, PIECES)),
                dma((2, chips, PIECES)),
                dma((2, chips - 1, PIECES)),
                dma((2, chips - 1, PIECES)),
                dma((2, chips, PIECES)),
                dma((2, chips, PIECES)),
            ],
            compiler_params=pltpu.CompilerParams(
                collective_id=0, has_side_effects=True, vmem_limit_bytes=46 * 2**20
            ),
        )(x, dy, gate, up, w_gate, w_up, w_down)
        return pl.pallas_call(
            store,
            name="store",
            out_shape=[jax.ShapeDtypeStruct(s, BF16) for s in shapes],
            in_specs=[VMEM] * 4,
            out_specs=[ANY] * 4,
            scratch_shapes=[dma((4,))],
            compiler_params=pltpu.CompilerParams(vmem_limit_bytes=2**20),
        )(*(pltpu.with_memory_space_constraint(o, pltpu.VMEM) for o in outs))

    tokens, columns, down = P("dp", None), P(None, "tp"), P("tp", None)
    return jax.shard_map(
        step,
        mesh=mesh,
        in_specs=(tokens, tokens, P("dp", "tp"), P("dp", "tp"), columns, columns, down),
        out_specs=(tokens, P("dp", "tp"), P("dp", "tp"), P(("dp", "tp"), None)),
        check_vma=False,
    )
```

time: 94.1 us -> 90.5 us (0.962)
  Pallas kernels: 93.2 us -> 89.6 us
    pallas_call x1, Pallas kernels: 87 us -> 83.4 us  [step(): pl.pallas_call(functools.partial(work, chips), name='work', out_shape=[pl...]
where the time goes in v2:
time: 90.5 us; the launch traced here: 90.4 us
  Pallas kernels  89.6 us (99%)
    pallas_call x1, Pallas kernels, step(): pl.pallas_call(functools.partial(work, chips), name='work', out_shape=[pl...  83.4 us
    pallas_call x1, Pallas kernels, step(): pl.pallas_call(store, name='store', out_shape=[jax.ShapeDtypeStruct(s, BF...  6.16 us

profile of v2, /device:TPU:113, one launch (start us, length us, event | category | flops | bytes accessed | tf_op | source)
XLA Modules:
  0.0 90.4 jit_solution(4998076384517430899)
XLA Ops:
  0.6 83.4 %work.1 = (bf16[2048,2048]{1,0:T(8,128)(2,1)S(1)}, bf16[2048,768]{1,0:T(8,128)(2,1)S(1)}, bf16[2048,768]{1,0:T(8,128)(2,1)S(1)}, bf16[768,2048]{1,0:T(8,128)(2,1)S(1)}) custom-call(bf16[2048,2048]{1,0:T(8,128)(2,1)} %x.1, bf16[2048,2048]{1,0:T(8,128)(2,1)} %dy.1, bf16[2048,768]{1,0:T(8,128)(2,1)} %gate.1, bf16[2048,768]{1,0:T(8,128)(2,1)} %up.1, ...), custom_call_target="tpu_custom_call" | custom-call | tf_op jit(solution)/shard_map/work/pallas_call | solution.py:314
  84.0 6.2 %store.1 = (bf16[2048,2048]{1,0:T(8,128)(2,1)}, bf16[2048,768]{1,0:T(8,128)(2,1)}, bf16[2048,768]{1,0:T(8,128)(2,1)}, bf16[768,2048]{1,0:T(8,128)(2,1)}) custom-call(bf16[2048,2048]{1,0:T(8,128)(2,1)S(1)} %get-tuple-element.8.refs_0_, bf16[2048,768]{1,0:T(8,128)(2,1)S(1)} %get-tuple-element.9.refs_1_, bf16[2048,768]{1,0:T(8,128)(2,1)S(1)} %get-tuple-element.10.refs_2_, ...), custom_call_target="tpu_custom_call" | custom-call | tf_op jit(solution)/shard_map/store/pallas_call | solution.py:347

commit v3 on v2

--- a/solution.py
+++ b/solution.py
@@ -29,13 +29,14 @@
     part = width // PIECES
     t = lax.axis_index("tp")
     k, c = t // 2, t % 2
-    right = {"tp": (k + 1) % chips * 2 + c}
-    left = {"tp": (k + chips - 1) % chips * 2 + c}
+    around = [k] + [(k + i) % chips for i in range(1, chips)]
+    right = {"tp": around[1] * 2 + c}
+    left = {"tp": around[-1] * 2 + c}
     partner = {"tp": k * 2 + 1 - c}
     ways = (right, left)
 
     def origin(d, hops):
-        return (k + chips - hops) % chips if d == 0 else (k + hops) % chips
+        return around[-hops] if d == 0 else around[hops]
 
     def row(chunk, d, core):
         return pl.multiple_of((chunk * 4 + d * 2 + core) * block, block)
@@ -55,7 +56,7 @@
         return 4 * (s * block + h * high(s))
 
     def segments(s, h):
-        todo = [(k + 2 * chips - 1 - s) % chips, (k + 1 + s) % chips]
+        todo = [around[-1 - s], around[(1 + s) % chips]]
         return [row(todo[d], d, core) + h * high(s) for core in (c, 1 - c) for d in (0, 1)]
 
     def load_dy(s, h):
@@ -94,7 +95,7 @@
 
     def start(copies):
         for copy in copies:
-            copy.start()
+            copy.start(priority=1)
 
     def weights_down(i):
         n = TILE // PIECES
@@ -119,10 +120,13 @@
     def remote(src, dst, send, recv, to):
         return pltpu.make_async_remote_copy(src_ref=src, dst_ref=dst, send_sem=send, recv_sem=recv, device_id=to)
 
+    def sent(like, sem):
+        pltpu.make_async_copy(like, like, sem).wait()
+
     def pair(s, h, q):
         at = (pl.ds(h * 2 * high(s), 2 * high(s)), pl.ds(q * part, part))
         u = number(s, h)
-        return remote(mate.at[s % 2, *at], got.at[s, *at], pair_s.at[u, q], pair_r.at[u, q], partner)
+        return remote(mate.at[s % 2, *at], got.at[s, *at], pair_s.at[s], pair_r.at[u, q], partner)
 
     def reduce(d, s, h, q):
         cols = pl.ds(q * part, part)
@@ -130,18 +134,18 @@
         return remote(
             got.at[s, pl.ds((h * 2 + d) * n, n), cols],
             ring.at[d, s, pl.ds(h * n, n), cols],
-            rs_s.at[d, u, q],
+            rs_s.at[0],
             rs_r.at[d, u, q],
             ways[d],
         )
 
     def gather(d, hops, q):
         at = dx.at[pl.ds(row(origin(d, hops), d, c), block), pl.ds(q * part, part)]
-        return remote(at, at, ag_s.at[d, hops, q], ag_r.at[d, hops, q], ways[d])
+        return remote(at, at, ag_s.at[0], ag_r.at[d, hops, q], ways[d])
 
     def share(d, hops, q):
         at = dx.at[pl.ds(row(origin(d, hops), d, c), block), pl.ds(q * part, part)]
-        return remote(at, at, fin_s.at[d, hops, q], fin_r.at[d, hops, q], partner)
+        return remote(at, at, fin_s.at[0], fin_r.at[0], partner)
 
     def pass_on(s, h, q):
         cols = pl.ds(q * part, part)
@@ -199,24 +203,32 @@
 
         for m, (src, dst) in enumerate(((gate, gs), (up, us))):
             pltpu.make_async_copy(src.at[pl.ds(0, 4 * n)], dst.at[s % 2, there], load.at[1 + m, u]).wait()
-        if u == 0:
+        if s == 0:
             for i in range(hidden // TILE):
                 silu, slope, _ = gates(i)
                 own[chips - 1, pl.ds(0, 4 * n), pl.ds(i * TILE, TILE)] = silu
                 own[chips - 1, pl.ds(0, 4 * n), pl.ds(hidden + i * TILE, TILE)] = slope
+            while waiting:
+                pass_on(*waiting.pop(0))
             pltpu.make_async_copy(dy.at[pl.ds(0, 4 * n)], dys.at[here], load.at[0, u]).wait()
-            for i in range(hidden // TILE):
-                wait_weights_down(i)
-                if i > 0:
-                    start(weights(i))
-                silu = own[chips - 1, pl.ds(0, 4 * n), pl.ds(i * TILE, TILE)]
-                slope = own[chips - 1, pl.ds(0, 4 * n), pl.ds(hidden + i * TILE, TILE)]
-                back(i, silu, slope, us[0, there, pl.ds(i * TILE, TILE)].astype(F32))
-            for q in range(hidden // TILE, PIECES):
-                start(weights(q))
+            if u == 0:
+                for i in range(hidden // TILE):
+                    wait_weights_down(i)
+                start(weights(1))
+            silu = own[chips - 1, pl.ds(0, 4 * n), pl.ds(0, hidden)]
+            slope = own[chips - 1, pl.ds(0, 4 * n), pl.ds(hidden, hidden)]
+            dh = dot(dys[here], wd[...], 1, 1)
+            dgu[here, pl.ds(0, hidden)] = (dh * us[0, there, :].astype(F32) * slope).astype(BF16)
+            dgu[here, pl.ds(hidden, hidden)] = (dh * silu).astype(BF16)
+            if u == 0:
+                for q in range(2, PIECES):
+                    start(weights(q))
         else:
             pltpu.make_async_copy(dy.at[pl.ds(0, 4 * n)], dys.at[here], load.at[0, u]).wait()
-            pl.loop(0, hidden // TILE)(lambda i: back(i, *gates(i)))
+            back(0, *gates(0))
+            while waiting:
+                pass_on(*waiting.pop(0))
+            pl.loop(1, hidden // TILE)(lambda i: back(i, *gates(i)))
         if u + 1 < len(units):
             load_dy(*units[u + 1])
             load_act(*units[u + 1])
@@ -225,9 +237,8 @@
             if u == 0:
                 for copy in weights(q):
                     copy.wait()
-            if s >= 2:
-                for before in halves(s - 2):
-                    pair(s - 2, before, q).wait_send()
+            if s >= 2 and q == 0:
+                sent(got.at[0], pair_s.at[s - 2])
             cols = pl.ds(q * part, part)
             v = dot(dgu[here, :], wgu[cols, :], 1, 1)
             mate[s % 2, pl.ds(h * 2 * n, 2 * n), cols] = v[2 * n :].astype(BF16)
@@ -275,19 +286,12 @@
     while events:
         forward(*events.pop(0))
 
-    for q in range(PIECES):
-        for s, h in units:
-            if s >= chips - 2:
-                pair(s, h, q).wait_send()
-            if s < chips - 1:
-                for d in (0, 1):
-                    reduce(d, s, h, q).wait_send()
-        for d in (0, 1):
-            for hops in range(chips - 1):
-                gather(d, hops, q).wait_send()
-            for hops in range(chips):
-                share(d, hops, q).wait_send()
-                share(d, hops, q).wait_recv()
+    for s in range(max(chips - 2, 0), chips):
+        sent(got.at[0], pair_s.at[s])
+    sent(dx.at[pl.ds(0, 2 * (chips - 1) * block)], rs_s.at[0])
+    sent(dx.at[pl.ds(0, 2 * (chips - 1) * block)], ag_s.at[0])
+    sent(dx.at[pl.ds(0, 2 * chips * block)], fin_s.at[0])
+    sent(dx.at[pl.ds(0, 2 * chips * block)], fin_r.at[0])
 
 
 def store(*refs):
@@ -331,14 +335,14 @@
                 dma((3, chips + 1)),
                 dma((3, PIECES)),
                 dma((PIECES,)),
+                dma((chips,)),
                 dma((chips + 1, PIECES)),
-                dma((chips + 1, PIECES)),
+                dma((1,)),
                 dma((2, chips, PIECES)),
-                dma((2, chips, PIECES)),
+                dma((1,)),
                 dma((2, chips - 1, PIECES)),
-                dma((2, chips - 1, PIECES)),
-                dma((2, chips, PIECES)),
-                dma((2, chips, PIECES)),
+                dma((1,)),
+                dma((1,)),
             ],
             compiler_params=pltpu.CompilerParams(
                 collective_id=0, has_side_effects=True, vmem_limit_bytes=46 * 2**20

time: 90.5 us -> 88.7 us (0.980)
  Pallas kernels: 89.6 us -> 87.8 us
    pallas_call x1, Pallas kernels: 83.4 us -> 81.6 us  [step(): pl.pallas_call(functools.partial(work, chips), name='work', out_shape=[pl...]
where the time goes in v3:
time: 88.7 us; the launch traced here: 88.6 us
  Pallas kernels  87.8 us (99%)
    pallas_call x1, Pallas kernels, step(): pl.pallas_call(functools.partial(work, chips), name='work', out_shape=[pl...  81.6 us
    pallas_call x1, Pallas kernels, step(): pl.pallas_call(store, name='store', out_shape=[jax.ShapeDtypeStruct(s, BF...  6.16 us

profile of v3, /device:TPU:113, one launch (start us, length us, event | category | flops | bytes accessed | tf_op | source)
XLA Modules:
  0.0 88.6 jit_solution(14281414306635961406)
XLA Ops:
  0.6 81.6 %work.1 = (bf16[2048,2048]{1,0:T(8,128)(2,1)S(1)}, bf16[2048,768]{1,0:T(8,128)(2,1)S(1)}, bf16[2048,768]{1,0:T(8,128)(2,1)S(1)}, bf16[768,2048]{1,0:T(8,128)(2,1)S(1)}) custom-call(bf16[2048,2048]{1,0:T(8,128)(2,1)} %x.1, bf16[2048,2048]{1,0:T(8,128)(2,1)} %dy.1, bf16[2048,768]{1,0:T(8,128)(2,1)} %gate.1, bf16[2048,768]{1,0:T(8,128)(2,1)} %up.1, ...), custom_call_target="tpu_custom_call" | custom-call | tf_op jit(solution)/shard_map/work/pallas_call | solution.py:318
  82.2 6.2 %store.1 = (bf16[2048,2048]{1,0:T(8,128)(2,1)}, bf16[2048,768]{1,0:T(8,128)(2,1)}, bf16[2048,768]{1,0:T(8,128)(2,1)}, bf16[768,2048]{1,0:T(8,128)(2,1)}) custom-call(bf16[2048,2048]{1,0:T(8,128)(2,1)S(1)} %get-tuple-element.8.refs_0_, bf16[2048,768]{1,0:T(8,128)(2,1)S(1)} %get-tuple-element.9.refs_1_, bf16[2048,768]{1,0:T(8,128)(2,1)S(1)} %get-tuple-element.10.refs_2_, ...), custom_call_target="tpu_custom_call" | custom-call | tf_op jit(solution)/shard_map/store/pallas_call | solution.py:351

commit v4 on v3

--- a/solution.py
+++ b/solution.py
@@ -11,6 +11,7 @@
 ANY = pl.BlockSpec(memory_space=pl.ANY)
 VMEM = pl.BlockSpec(memory_space=pltpu.VMEM)
 PIECES = 4
+SPLIT = 2
 TILE = 256
 
 
@@ -41,13 +42,22 @@
     def row(chunk, d, core):
         return pl.multiple_of((chunk * 4 + d * 2 + core) * block, block)
 
-    units = [(0, 0), (0, 1)] + [(s, 0) for s in range(1, chips)]
+    split = min(SPLIT, chips - 1)
+    units = [(s, h) for s in range(split) for h in (0, 1)] + [(s, 0) for s in range(split, chips)]
+
+    quarters, halves_of = [(q * part, part) for q in range(PIECES)], [(0, width // 2), (width // 2, width // 2)]
+    pair_cuts = [[(0, part // 2), (part // 2, part // 2), *quarters[1:]]] + [quarters] * (len(units) - 1)
+    sum_cuts = pair_cuts[: 2 * split] + [halves_of if s > 2 else quarters for s in range(split, chips)]
+    gather_cuts = [halves_of] * (chips - 2) + [quarters]
+
+    def within(cut, cuts):
+        return [i for i, (a, n) in enumerate(cuts) if cut[0] <= a and a + n <= cut[0] + cut[1]]
 
     def high(s):
-        return block // 2 if s == 0 else block
+        return block // 2 if s < split else block
 
     def halves(s):
-        return (0, 1) if s == 0 else (0,)
+        return (0, 1) if s < split else (0,)
 
     def number(s, h):
         return units.index((s, h))
@@ -123,62 +133,74 @@
     def sent(like, sem):
         pltpu.make_async_copy(like, like, sem).wait()
 
-    def pair(s, h, q):
-        at = (pl.ds(h * 2 * high(s), 2 * high(s)), pl.ds(q * part, part))
+    def pair(s, h, i):
         u = number(s, h)
-        return remote(mate.at[s % 2, *at], got.at[s, *at], pair_s.at[s], pair_r.at[u, q], partner)
-
-    def reduce(d, s, h, q):
-        cols = pl.ds(q * part, part)
+        at = (pl.ds(h * 2 * high(s), 2 * high(s)), pl.ds(*pair_cuts[u][i]))
+        return remote(mate.at[s % 2, *at], got.at[s, *at], pair_s.at[s], pair_r.at[u, i], partner)
+
+    def reduce(d, s, h, i):
         n, u = high(s), number(s, h)
+        cols = pl.ds(*sum_cuts[u][i])
         return remote(
             got.at[s, pl.ds((h * 2 + d) * n, n), cols],
             ring.at[d, s, pl.ds(h * n, n), cols],
             rs_s.at[0],
-            rs_r.at[d, u, q],
+            rs_r.at[d, u, i],
             ways[d],
         )
 
-    def gather(d, hops, q):
-        at = dx.at[pl.ds(row(origin(d, hops), d, c), block), pl.ds(q * part, part)]
-        return remote(at, at, ag_s.at[0], ag_r.at[d, hops, q], ways[d])
-
-    def share(d, hops, q):
-        at = dx.at[pl.ds(row(origin(d, hops), d, c), block), pl.ds(q * part, part)]
+    def gather(d, hops, i):
+        at = dx.at[pl.ds(row(origin(d, hops), d, c), block), pl.ds(*gather_cuts[hops][i])]
+        return remote(at, at, ag_s.at[0], ag_r.at[d, hops, i], ways[d])
+
+    def share(d, hops, cut):
+        at = dx.at[pl.ds(row(origin(d, hops), d, c), block), pl.ds(*cut)]
         return remote(at, at, fin_s.at[0], fin_r.at[0], partner)
 
-    def pass_on(s, h, q):
-        cols = pl.ds(q * part, part)
-        n = high(s)
-        pair(s, h, q).wait_recv()
+    def pass_on(s, h, i):
+        n, u = high(s), number(s, h)
+        cut = sum_cuts[u][i]
+        cols = pl.ds(*cut)
+        for j in within(cut, pair_cuts[u]):
+            pair(s, h, j).wait_recv()
         for d in (0, 1):
             band = pl.ds((h * 2 + d) * n, n)
             total = own[s, band, cols] + got[s, band, cols].astype(F32)
             if s > 0:
-                for before in halves(s - 1):
-                    reduce(d, s - 1, before, q).wait_recv()
-                total = total + ring[d, s - 1, :, cols].astype(F32)
+                for before in (h,) if s < split else halves(s - 1):
+                    for j in within(cut, sum_cuts[number(s - 1, before)]):
+                        reduce(d, s - 1, before, j).wait_recv()
+                total = total + ring[d, s - 1, pl.ds(h * n, n), cols].astype(F32)
             if s < chips - 1:
                 got[s, band, cols] = total.astype(BF16)
             else:
                 dx[pl.ds(row(k, d, c), block), cols] = total.astype(BF16)
         for d in (0, 1):
             if s < chips - 1:
-                reduce(d, s, h, q).start()
+                reduce(d, s, h, i).start()
             else:
-                gather(d, 0, q).start()
+                for j in within(cut, gather_cuts[0]):
+                    gather(d, 0, j).start()
         if s == chips - 1:
             for d in (0, 1):
-                share(d, 0, q).start()
-
-    def forward(hops, q):
+                share(d, 0, cut).start()
+
+    def forward(hops, i):
+        cut = gather_cuts[hops - 1][i]
         for d in (0, 1):
-            gather(d, hops - 1, q).wait_recv()
+            gather(d, hops - 1, i).wait_recv()
             if hops < chips - 1:
-                gather(d, hops, q).start()
-            share(d, hops, q).start()
+                for j in within(cut, gather_cuts[hops]):
+                    gather(d, hops, j).start()
+            share(d, hops, cut).start()
 
     waiting = []
+
+    def flush(lag=0):
+        while waiting and begun[0] - waiting[0][1] >= lag:
+            pass_on(*waiting.pop(0)[0])
+
+    begun = [0]
     for s, h in units:
         n = high(s)
         here = pl.ds(begin(s, h), 4 * n)
@@ -203,13 +225,12 @@
 
         for m, (src, dst) in enumerate(((gate, gs), (up, us))):
             pltpu.make_async_copy(src.at[pl.ds(0, 4 * n)], dst.at[s % 2, there], load.at[1 + m, u]).wait()
-        if s == 0:
+        if s < split:
             for i in range(hidden // TILE):
                 silu, slope, _ = gates(i)
                 own[chips - 1, pl.ds(0, 4 * n), pl.ds(i * TILE, TILE)] = silu
                 own[chips - 1, pl.ds(0, 4 * n), pl.ds(hidden + i * TILE, TILE)] = slope
-            while waiting:
-                pass_on(*waiting.pop(0))
+            flush()
             pltpu.make_async_copy(dy.at[pl.ds(0, 4 * n)], dys.at[here], load.at[0, u]).wait()
             if u == 0:
                 for i in range(hidden // TILE):
@@ -218,7 +239,7 @@
             silu = own[chips - 1, pl.ds(0, 4 * n), pl.ds(0, hidden)]
             slope = own[chips - 1, pl.ds(0, 4 * n), pl.ds(hidden, hidden)]
             dh = dot(dys[here], wd[...], 1, 1)
-            dgu[here, pl.ds(0, hidden)] = (dh * us[0, there, :].astype(F32) * slope).astype(BF16)
+            dgu[here, pl.ds(0, hidden)] = (dh * us[s % 2, there, :].astype(F32) * slope).astype(BF16)
             dgu[here, pl.ds(hidden, hidden)] = (dh * silu).astype(BF16)
             if u == 0:
                 for q in range(2, PIECES):
@@ -226,36 +247,36 @@
         else:
             pltpu.make_async_copy(dy.at[pl.ds(0, 4 * n)], dys.at[here], load.at[0, u]).wait()
             back(0, *gates(0))
-            while waiting:
-                pass_on(*waiting.pop(0))
+            flush()
             pl.loop(1, hidden // TILE)(lambda i: back(i, *gates(i)))
         if u + 1 < len(units):
             load_dy(*units[u + 1])
             load_act(*units[u + 1])
 
-        for q in range(PIECES):
-            if u == 0:
-                for copy in weights(q):
+        for i, cut in enumerate(pair_cuts[u]):
+            if u == 0 and cut[0] % part == 0:
+                for copy in weights(cut[0] // part):
                     copy.wait()
-            if s >= 2 and q == 0:
+            if s >= 2 and h == 0 and i == 0:
                 sent(got.at[0], pair_s.at[s - 2])
-            cols = pl.ds(q * part, part)
+            cols = pl.ds(*cut)
             v = dot(dgu[here, :], wgu[cols, :], 1, 1)
             mate[s % 2, pl.ds(h * 2 * n, 2 * n), cols] = v[2 * n :].astype(BF16)
-            if u == 0 and q == 0:
+            if u == 0 and i == 0:
                 pl.semaphore_wait(barrier, 3)
-            pair(s, h, q).start()
+            pair(s, h, i).start()
             own[s, pl.ds(h * 2 * n, 2 * n), cols] = v[: 2 * n]
-            waiting.append((s, h, q))
-            while len(waiting) > (2 if s == 0 else 1):
-                pass_on(*waiting.pop(0))
+            begun[0] += 1
+            for j, whole in enumerate(sum_cuts[u]):
+                if within(whole, pair_cuts[u])[-1] == i:
+                    waiting.append(((s, h, j), begun[0]))
+            flush(2 if s < split else 1)
         if (s, h) == units[-1]:
             load_x(0)
             load_x(1)
-    while waiting:
-        pass_on(*waiting.pop(0))
-
-    events = [(hops, q) for hops in range(1, chips) for q in range(PIECES)]
+    flush()
+
+    events = [(hops, i) for hops in range(1, chips) for i in range(len(gather_cuts[hops - 1]))]
 
     for b in range(PIECES):
         band = pl.ds(b * part, part)
@@ -266,7 +287,7 @@
             cols = pl.ds(pl.multiple_of(b * part + i * TILE, TILE), TILE)
             wd[:, cols] = dot(hid[...], dys[:, cols], 0, 0).astype(BF16)
 
-        if b > 0:
+        if b == PIECES - 1:
             forward(*events.pop(0))
         pltpu.make_async_copy(x.at[:, band], wgu.at[:, slot], xload.at[b]).wait()
 
@@ -278,7 +299,7 @@
                 from_cols = pl.ds(pl.multiple_of(m * hidden + i * TILE, TILE), TILE)
                 out[band, cols] = dot(wgu[:, slot], dgu[:, from_cols], 0, 0).astype(BF16)
 
-            if m == 0:
+            if (b, m) in ((0, 1), (1, 0), (2, 0)):
                 forward(*events.pop(0))
         if b + 2 < PIECES:
             load_x(b + 2)
@@ -332,13 +353,13 @@
                 pltpu.VMEM((2, 4 * block, hidden), BF16),
                 pltpu.VMEM((2, 4 * block, hidden), BF16),
                 pltpu.VMEM((width, 2 * hidden), BF16),
-                dma((3, chips + 1)),
+                dma((3, chips + SPLIT)),
                 dma((3, PIECES)),
                 dma((PIECES,)),
                 dma((chips,)),
-                dma((chips + 1, PIECES)),
+                dma((chips + SPLIT, PIECES + 1)),
                 dma((1,)),
-                dma((2, chips, PIECES)),
+                dma((2, chips + SPLIT - 1, PIECES + 1)),
                 dma((1,)),
                 dma((2, chips - 1, PIECES)),
                 dma((1,)),

time: 88.7 us -> 88.2 us (level)
  no operation moved by 1% of the time
where the time goes in v4:
time: 88.2 us; the launch traced here: 88.1 us
  Pallas kernels  87.3 us (99%)
    pallas_call x1, Pallas kernels, step(): pl.pallas_call(functools.partial(work, chips), name='work', out_shape=[pl...  81.1 us
    pallas_call x1, Pallas kernels, step(): pl.pallas_call(store, name='store', out_shape=[jax.ShapeDtypeStruct(s, BF...  6.16 us

profile of v4, /device:TPU:113, one launch (start us, length us, event | category | flops | bytes accessed | tf_op | source)
XLA Modules:
  0.0 88.1 jit_solution(16149175982979590417)
XLA Ops:
  0.6 81.1 %work.1 = (bf16[2048,2048]{1,0:T(8,128)(2,1)S(1)}, bf16[2048,768]{1,0:T(8,128)(2,1)S(1)}, bf16[2048,768]{1,0:T(8,128)(2,1)S(1)}, bf16[768,2048]{1,0:T(8,128)(2,1)S(1)}) custom-call(bf16[2048,2048]{1,0:T(8,128)(2,1)} %x.1, bf16[2048,2048]{1,0:T(8,128)(2,1)} %dy.1, bf16[2048,768]{1,0:T(8,128)(2,1)} %gate.1, bf16[2048,768]{1,0:T(8,128)(2,1)} %up.1, ...), custom_call_target="tpu_custom_call" | custom-call | tf_op jit(solution)/shard_map/work/pallas_call | solution.py:339
  81.8 6.2 %store.1 = (bf16[2048,2048]{1,0:T(8,128)(2,1)}, bf16[2048,768]{1,0:T(8,128)(2,1)}, bf16[2048,768]{1,0:T(8,128)(2,1)}, bf16[768,2048]{1,0:T(8,128)(2,1)}) custom-call(bf16[2048,2048]{1,0:T(8,128)(2,1)S(1)} %get-tuple-element.8.refs_0_, bf16[2048,768]{1,0:T(8,128)(2,1)S(1)} %get-tuple-element.9.refs_1_, bf16[2048,768]{1,0:T(8,128)(2,1)S(1)} %get-tuple-element.10.refs_2_, ...), custom_call_target="tpu_custom_call" | custom-call | tf_op jit(solution)/shard_map/store/pallas_call | solution.py:372

commit v5 on v4

--- a/solution.py
+++ b/solution.py
@@ -12,6 +12,7 @@
 VMEM = pl.BlockSpec(memory_space=pltpu.VMEM)
 PIECES = 4
 SPLIT = 2
+STORES = 16
 TILE = 256
 
 
@@ -48,7 +49,8 @@
     quarters, halves_of = [(q * part, part) for q in range(PIECES)], [(0, width // 2), (width // 2, width // 2)]
     pair_cuts = [[(0, part // 2), (part // 2, part // 2), *quarters[1:]]] + [quarters] * (len(units) - 1)
     sum_cuts = pair_cuts[: 2 * split] + [halves_of if s > 2 else quarters for s in range(split, chips)]
-    gather_cuts = [halves_of] * (chips - 2) + [quarters]
+    last = [(0, 2 * part), (2 * part, part), (3 * part, part // 2), (3 * part + part // 2, part // 2)]
+    gather_cuts = [halves_of] * (chips - 2) + [last]
 
     def within(cut, cuts):
         return [i for i, (a, n) in enumerate(cuts) if cut[0] <= a and a + n <= cut[0] + cut[1]]
@@ -74,7 +76,7 @@
         for i, r in enumerate(segments(s, h)):
             pltpu.make_async_copy(
                 dy.at[pl.ds(r, n)], dys.at[pl.ds(begin(s, h) + i * n, n)], load.at[0, number(s, h)]
-            ).start()
+            ).start(priority=0 if (s, h) == (0, 0) else 1)
 
     def load_act(s, h):
         n = high(s)
@@ -84,7 +86,7 @@
                     src.at[pl.ds(r, n)],
                     dst.at[s % 2, pl.ds((h * 4 + i) * n, n)],
                     load.at[1 + m, number(s, h)],
-                ).start()
+                ).start(priority=0 if (s, h) == (0, 0) else 1)
 
     def load_x(b):
         for s, h in units:
@@ -94,7 +96,7 @@
                     x.at[pl.ds(r, n), pl.ds(b * part, part)],
                     wgu.at[pl.ds(begin(s, h) + i * n, n), pl.ds(b % 2 * part, part)],
                     xload.at[b],
-                ).start()
+                ).start(priority=1)
 
     def weights(q):
         band = pl.ds(q * part, part)
@@ -319,8 +321,8 @@
     n = (len(refs) - 1) // 2
     sems = refs[-1]
     for i, (src, dst) in enumerate(zip(refs[:n], refs[n:-1])):
-        size = src.shape[0] // PIECES
-        for p in range(PIECES):
+        size = src.shape[0] // STORES
+        for p in range(STORES):
             at = pl.ds(p * size, size)
             pltpu.make_async_copy(src.at[at], dst.at[at], sems.at[i]).start()
     for i, (src, dst) in enumerate(zip(refs[:n], refs[n:-1])):

time: 88.2 us -> 87.9 us (level)
  no operation moved by 1% of the time
where the time goes in v5:
time: 87.9 us
  Pallas kernels  87 us (99%)
    pallas_call x1, Pallas kernels, step(): pl.pallas_call(functools.partial(work, chips), name='work', out_shape=[pl...  80.9 us
    pallas_call x1, Pallas kernels, step(): pl.pallas_call(store, name='store', out_shape=[jax.ShapeDtypeStruct(s, BF...  6.12 us

profile of v5, /device:TPU:113, one launch (start us, length us, event | category | flops | bytes accessed | tf_op | source)
XLA Modules:
  0.0 87.9 jit_solution(6809684057822317837)
XLA Ops:
  0.6 80.9 %work.1 = (bf16[2048,2048]{1,0:T(8,128)(2,1)S(1)}, bf16[2048,768]{1,0:T(8,128)(2,1)S(1)}, bf16[2048,768]{1,0:T(8,128)(2,1)S(1)}, bf16[768,2048]{1,0:T(8,128)(2,1)S(1)}) custom-call(bf16[2048,2048]{1,0:T(8,128)(2,1)} %x.1, bf16[2048,2048]{1,0:T(8,128)(2,1)} %dy.1, bf16[2048,768]{1,0:T(8,128)(2,1)} %gate.1, bf16[2048,768]{1,0:T(8,128)(2,1)} %up.1, ...), custom_call_target="tpu_custom_call" | custom-call | tf_op jit(solution)/shard_map/work/pallas_call | solution.py:341
  81.6 6.1 %store.1 = (bf16[2048,2048]{1,0:T(8,128)(2,1)}, bf16[2048,768]{1,0:T(8,128)(2,1)}, bf16[2048,768]{1,0:T(8,128)(2,1)}, bf16[768,2048]{1,0:T(8,128)(2,1)}) custom-call(bf16[2048,2048]{1,0:T(8,128)(2,1)S(1)} %get-tuple-element.8.refs_0_, bf16[2048,768]{1,0:T(8,128)(2,1)S(1)} %get-tuple-element.9.refs_1_, bf16[2048,768]{1,0:T(8,128)(2,1)S(1)} %get-tuple-element.10.refs_2_, ...), custom_call_target="tpu_custom_call" | custom-call | tf_op jit(solution)/shard_map/store/pallas_call | solution.py:374

commit v6 on v5

--- a/solution.py
+++ b/solution.py
@@ -250,7 +250,8 @@
             pltpu.make_async_copy(dy.at[pl.ds(0, 4 * n)], dys.at[here], load.at[0, u]).wait()
             back(0, *gates(0))
             flush()
-            pl.loop(1, hidden // TILE)(lambda i: back(i, *gates(i)))
+            for i in range(1, hidden // TILE):
+                back(i, *gates(i))
         if u + 1 < len(units):
             load_dy(*units[u + 1])
             load_act(*units[u + 1])

time: 87.9 us -> 87.9 us (level)
  no operation moved by 1% of the time
where the time goes in v6:
time: 87.9 us
  Pallas kernels  87 us (99%)
    pallas_call x1, Pallas kernels, step(): pl.pallas_call(functools.partial(work, chips), name='work', out_shape=[pl...  80.9 us
    pallas_call x1, Pallas kernels, step(): pl.pallas_call(store, name='store', out_shape=[jax.ShapeDtypeStruct(s, BF...  6.12 us

profile of v6, /device:TPU:113, one launch (start us, length us, event | category | flops | bytes accessed | tf_op | source)
XLA Modules:
  0.0 87.9 jit_solution(17826527958111825625)
XLA Ops:
  0.6 80.9 %work.1 = (bf16[2048,2048]{1,0:T(8,128)(2,1)S(1)}, bf16[2048,768]{1,0:T(8,128)(2,1)S(1)}, bf16[2048,768]{1,0:T(8,128)(2,1)S(1)}, bf16[768,2048]{1,0:T(8,128)(2,1)S(1)}) custom-call(bf16[2048,2048]{1,0:T(8,128)(2,1)} %x.1, bf16[2048,2048]{1,0:T(8,128)(2,1)} %dy.1, bf16[2048,768]{1,0:T(8,128)(2,1)} %gate.1, bf16[2048,768]{1,0:T(8,128)(2,1)} %up.1, ...), custom_call_target="tpu_custom_call" | custom-call | tf_op jit(solution)/shard_map/work/pallas_call | solution.py:342
  81.6 6.1 %store.1 = (bf16[2048,2048]{1,0:T(8,128)(2,1)}, bf16[2048,768]{1,0:T(8,128)(2,1)}, bf16[2048,768]{1,0:T(8,128)(2,1)}, bf16[768,2048]{1,0:T(8,128)(2,1)}) custom-call(bf16[2048,2048]{1,0:T(8,128)(2,1)S(1)} %get-tuple-element.8.refs_0_, bf16[2048,768]{1,0:T(8,128)(2,1)S(1)} %get-tuple-element.9.refs_1_, bf16[2048,768]{1,0:T(8,128)(2,1)S(1)} %get-tuple-element.10.refs_2_, ...), custom_call_target="tpu_custom_call" | custom-call | tf_op jit(solution)/shard_map/store/pallas_call | solution.py:375
